TPU v7x, 32 devices: a whole 2x2x4 slice. The times are simulated.
32 devices in a mesh: cell: 8 (over z, y), pool: 4 (over x, core).
Axes of the slice: x: 2, y: 2, z: 4, core: 2. Of those that a mesh axis runs over, the one named last changes fastest.
Arguments:
- fractions: bfloat16 [256, 8192], P(None, 'cell'), may hold values from 0 to 1, as said below
- order: int32 [8192], P('cell'), may hold values from 0 to 8191, as said below
- density: float32 [8, 16, 8192], P('pool', None, 'cell'), may hold values from 0.2 to 5
- area: float32 [16, 8192], P(None, 'cell'), may hold values from 0.05 to 3
- harvest: float32 [8], P('pool'), may hold values from 0.05 to 0.6
Outputs:
- new_density: float32 [8, 16, 8192], P('pool', None, 'cell')
- area_cum: float32 [16, 8192], P(None, 'cell')
- stock_mean: float32 [8, 16], P('pool')
- removed: float32 [16], replicated
Inputs may be any that keep to these rules, and one draw needn't show every extreme that they name: A permutation of the cells; of the cells that one device holds in region order, every gridcell block of 1024 positions receives the same number. `fractions`: each column of a cell's matrix sums to one before rounding, with diagonal entries of 0.4 or more.
All inputs are finite; a program needn't handle non-finite values.
Results may differ from a plain program's by a relative error of at most 0.0003.
Values may be sent and summed in bfloat16 or wider, within the bound.
No kernel may reach another device: no remote copies, remote signals or barrier semaphores. Data moves between devices by JAX's collectives and lax.ppermute only.
A program may use at most 64 MiB of HBM per device.

v0:
```python
import functools

import jax
import jax.numpy as jnp
from jax import lax
from jax.experimental import pallas as pl
from jax.experimental.pallas import tpu as pltpu
from jax.sharding import PartitionSpec as P


LANES = 128
VMEM_LIMIT = 16 * 1024 * 1024
NT = (((1,), (1,)), ((), ()))
NN = (((1,), (0,)), ((), ()))
F32 = jnp.float32
BF16 = jnp.bfloat16


def iota(shape, dim):
    return lax.broadcasted_iota(jnp.int32, shape, dim)


def pack_kernel(*refs, even, odd):
    count = 1 + len(even)
    sources, (*out_refs, weighted_out), loaded, arrived = refs[:5], refs[5:6 + count], refs[6 + count:-1], refs[-1]
    order_vmem, frac, harvest, density, area = loaded
    copies = [
        pltpu.make_async_copy(source, target, arrived.at[n])
        for n, (source, target) in enumerate(zip(sources, loaded))
    ]
    for copy in copies:
        copy.start()
    _, owned = frac.shape
    blocks = owned // LANES
    rows = -(-count // 8) * 8
    cell = lax.axis_index("cell")
    core = lax.rem(lax.axis_index("pool"), 2)
    want = jnp.where(iota((rows, LANES), 0) == 0, cell, -1)
    for k, a in enumerate(even):
        target = cell ^ jnp.where(core == 0, a, odd[k] if k < len(odd) else 0)
        want = jnp.where(iota((rows, LANES), 0) == k + 1, target, want)
    sums = jnp.where(iota((LANES, 2 * LANES), 0) < iota((LANES, 2 * LANES), 1), 1.0, 0.0).astype(BF16)
    copies[0].wait()
    order = order_vmem[...]
    dest = lax.shift_right_logical(order, owned.bit_length() - 1)
    local = order & (owned - 1)
    hits = [dest[:, b * LANES:(b + 1) * LANES] == want for b in range(blocks)]
    ones = jnp.concatenate([jnp.where(h, 1.0, 0.0) for h in hits], axis=0).astype(BF16)
    prefix = lax.dot_general(ones, sums, NN, preferred_element_type=F32)
    before = jnp.zeros((rows, LANES), F32)
    slots = []
    for b in range(blocks):
        part = prefix[b * rows:(b + 1) * rows]
        slots.append(jnp.where(hits[b], part[:, :LANES] + before, -1.0))
        before = before + part[:, LANES:]
    slots = jnp.concatenate(slots, axis=1)
    width = out_refs[0].shape[1]
    onehot = jnp.concatenate([matches(slots[k:k + 1], width) for k in range(count)], axis=0)
    high = lax.shift_right_logical(local, 7).astype(F32)
    low = (local & (LANES - 1)).astype(F32)
    which = iota((16, owned), 0)
    extra = jnp.where(which == 0, high, jnp.where(which == 1, low, 0.0)).astype(BF16)
    for copy in copies[2:]:
        copy.wait()
    pools = density.shape[0]
    weighted_out[...] = area[...] * sum(harvest[:, p:p + 1] * density[p] for p in range(pools))
    copies[1].wait()
    data = jnp.concatenate([frac[...], extra], axis=0)
    packed = lax.dot_general(data, onehot, NT, preferred_element_type=F32).astype(BF16)
    for k in range(count):
        out_refs[k][...] = packed[:, k * width:(k + 1) * width]


def matches(row, height):
    steps = iota((height, row.shape[1]), 0).astype(F32).astype(BF16)
    one = jnp.ones(steps.shape, BF16)
    return jnp.where(steps == row.astype(BF16), one, jnp.zeros_like(one))


def placed(parts, kinds, owned):
    data = jnp.concatenate(parts, axis=1)
    tail = data[kinds:].astype(F32)
    high, low = tail[0:1], tail[1:2]
    onehot = jnp.concatenate(
        [matches(jnp.where(high == b, low, -1.0), LANES) for b in range(owned // LANES)], axis=0
    )
    return lax.dot_general(data[:kinds], onehot, NT, preferred_element_type=F32)


def place_kernel(*refs):
    kinds, owned = refs[-1].shape
    refs[-1][...] = placed([ref[...] for ref in refs[:-1]], kinds, owned).astype(BF16)


def transition_kernel(harvest_ref, density_ref, area_ref, weighted_a, weighted_b, early_ref, *refs, parts):
    stock_out, area_out, sums_out, block = refs[parts:]
    pools, types, owned = density_ref.shape
    kinds = types * types
    blocks = owned // LANES
    last = [ref[...] for ref in refs[:parts]]
    late = placed(last[:-2] + [last[-2] + last[-1]], kinds, owned) + early_ref[...].astype(F32)
    for b in range(blocks):
        block[b * kinds:(b + 1) * kinds] = late[:, b * LANES:(b + 1) * LANES]
    dest = iota((types, LANES), 0)
    sums = [jnp.zeros((types, LANES), F32) for _ in range(pools + 1)]
    for b in range(blocks):
        at = slice(b * LANES, (b + 1) * LANES)
        area = area_ref[:, at]
        stock = [area * density_ref[p, :, at] for p in range(pools)]
        sources = stock + [weighted_a[:, at] + weighted_b[:, at], area]
        totals = [jnp.zeros((types, LANES), F32) for _ in sources]
        staying = jnp.zeros((types, LANES), F32)
        for j in range(types):
            column = block[pl.ds(b * kinds + j, types, stride=types), :]
            staying = jnp.where(dest == j, column, staying)
            totals = [t + column * s[j:j + 1] for t, s in zip(totals, sources)]
        for p in range(pools):
            kept = staying * stock[p]
            new_stock = kept + (1.0 - harvest_ref[:, p:p + 1]) * (totals[p] - kept)
            stock_out[p, :, at] = new_stock
            sums[p] = sums[p] + new_stock
        sums[pools] = sums[pools] + (totals[pools] - staying * sources[pools])
        area_out[:, at] = totals[-1]
    diagonal = dest == iota((types, LANES), 1)
    rows = []
    for s in sums:
        each = jnp.sum(s, axis=1, keepdims=True)
        rows.append(jnp.sum(jnp.where(diagonal, each, 0.0), axis=0, keepdims=True))
    rows.append(jnp.zeros((sums_out.shape[0] - len(rows), LANES), F32))
    sums_out[...] = jnp.concatenate(rows, axis=0)


def density_kernel(stock_ref, area_ref, density_out, cum_out):
    pools, types, owned = stock_ref.shape
    running = area_ref[...]
    inverse = 1.0 / running
    for p in range(pools):
        density_out[p] = stock_ref[p] * inverse
    dest = iota((types, owned), 0)
    step = 1
    while step < types:
        running = running + jnp.where(dest >= step, pltpu.roll(running, step, 0), 0.0)
        step *= 2
    cum_out[...] = running / running[types - 1:types]


def finish_kernel(sums_a, sums_b, mean_out, removed_out, *, scale):
    pools, types = mean_out.shape
    sums = (sums_a[...] + sums_b[...]) * scale
    mean_out[...] = sums[:pools, :types]
    removed_out[...] = sums[pools:pools + 1, :types]


def call(kernel, out_shape, args, scratch=(), cost=None, space=pltpu.VMEM):
    vmem = pl.BlockSpec(memory_space=pltpu.VMEM)
    return pl.pallas_call(
        kernel,
        out_shape=out_shape,
        in_specs=[pl.BlockSpec(memory_space=space)] * len(args),
        out_specs=jax.tree.map(lambda _: vmem, out_shape),
        scratch_shapes=list(scratch),
        compiler_params=pltpu.CompilerParams(vmem_limit_bytes=VMEM_LIMIT),
        cost_estimate=cost,
    )(*args)


def array(*shape, dtype=F32):
    return jax.ShapeDtypeStruct(shape, dtype)


def fast_body(cells, pools_axis, fractions, order, density, area, harvest):
    kinds, owned = fractions.shape
    pools, types, _ = density.shape
    chunk = owned // cells
    even, odd = SPLIT[cells]
    count = 1 + len(even)
    harvest = harvest.reshape(1, pools)
    sources = (order.reshape(1, owned), fractions, harvest, density, area)
    *packed, weighted = call(
        functools.partial(pack_kernel, even=even, odd=odd),
        [array(kinds + 16, chunk, dtype=BF16)] * count + [array(types, owned)],
        [pltpu.with_memory_space_constraint(x, pltpu.HBM) for x in sources],
        scratch=[pltpu.VMEM(x.shape, x.dtype) for x in sources] + [pltpu.SemaphoreType.DMA((len(sources),))],
        space=pltpu.HBM,
    )
    received = []
    for k, a in enumerate(even):
        b = odd[k] if k < len(odd) else None
        pairs = []
        for c in range(cells):
            for p in range(pools_axis):
                s = a if p % 2 == 0 else b
                if s is not None:
                    pairs.append((c * pools_axis + p, (c ^ s) * pools_axis + p))
        received.append(lax.ppermute(packed[1 + k], ("cell", "pool"), pairs))
    other = []
    for r in received:
        other.append(swap(r, "pool", pools_axis, 1))
    step = 1
    while step < pools_axis // 2:
        weighted = weighted + swap(weighted, "pool", pools_axis, step)
        step *= 2
    weighted_far = swap(weighted, "pool", pools_axis, step)
    early = [packed[0]] + received[:-1] + other[:-2]
    placed_early = call(
        place_kernel,
        array(kinds, owned, dtype=BF16),
        early,
        cost=pl.CostEstimate(flops=2 * kinds * owned * owned, bytes_accessed=2 * kinds * owned, transcendentals=0),
    )
    late = [other[-2], received[-1], other[-1]]
    new_stock, new_area, sums = call(
        functools.partial(transition_kernel, parts=len(late)),
        [array(pools, types, owned), array(types, owned), array(8, LANES)],
        (harvest, density, area, weighted, weighted_far, placed_early, *late),
        scratch=[pltpu.VMEM((kinds * (owned // LANES), LANES), F32)],
    )
    new_density, area_cum = call(
        density_kernel, [array(pools, types, owned), array(types, owned)], (new_stock, new_area)
    )
    step = 1
    while step < cells // 2:
        sums = sums + swap(sums, "cell", cells, step)
        step *= 2
    last = swap(sums, "cell", cells, step)
    mean, removed = call(
        functools.partial(finish_kernel, scale=1.0 / (cells * owned)),
        [array(pools, types), array(1, types)],
        (sums, last),
    )
    return new_density, area_cum, mean, removed.reshape(types)


def swap(value, axis, size, step):
    return lax.ppermute(value, axis, [(n, n ^ step) for n in range(size)])


SPLIT = {8: ((6, 4, 2, 1), (7, 5, 3))}


def place_columns(received, positions, owned):
    local = positions[0] - lax.axis_index("cell") * owned
    inverse = jnp.zeros((owned,), jnp.int32).at[local].set(jnp.arange(owned, dtype=jnp.int32))
    return jnp.take(received, inverse, axis=1)


def general_body(fractions, order, density, area, harvest):
    owned = fractions.shape[1]
    types = area.shape[0]
    grouping = jnp.argsort(order // owned, stable=True)
    positions = jnp.take(order, grouping).reshape(1, owned)
    outgoing = jnp.take(fractions, grouping, axis=1)
    received, got_pos = (
        lax.all_to_all(outgoing, "cell", split_axis=1, concat_axis=1, tiled=True),
        lax.all_to_all(positions, "cell", split_axis=1, concat_axis=1, tiled=True),
    )
    block_frac = place_columns(received, got_pos, owned)
    matrix = block_frac.astype(F32).reshape(types, types, owned)
    stock = area[None] * density
    total = jnp.einsum("ijc,pjc->pic", matrix, stock, precision=lax.Precision.HIGHEST)
    staying = block_frac.astype(F32)[:: types + 1]
    moved = total - staying[None] * stock
    new_stock = staying[None] * stock + (1.0 - harvest[:, None, None]) * moved
    new_area = jnp.einsum("ijc,jc->ic", matrix, area, precision=lax.Precision.HIGHEST)
    new_density = new_stock / new_area[None]
    area_cum = jnp.cumsum(new_area, axis=0) / jnp.sum(new_area, axis=0, keepdims=True)
    stock_local = jnp.sum(new_stock, axis=2)
    removed_local = jnp.sum(harvest[:, None, None] * moved, axis=(0, 2))
    stock_sums, removed_cells = lax.psum((stock_local, removed_local), "cell")
    removed_sums = lax.psum(removed_cells, "pool")
    count = lax.axis_size("cell") * owned
    return (new_density, area_cum, stock_sums / count, removed_sums / count)


def solution(mesh):
    cells, pools_axis = mesh.shape["cell"], mesh.shape["pool"]

    def body(fractions, order, density, area, harvest):
        _, owned = fractions.shape
        types = area.shape[0]
        fits = (
            cells in SPLIT
            and pools_axis & (pools_axis - 1) == 0
            and pools_axis > 1
            and owned & (owned - 1) == 0
            and owned % (cells * LANES) == 0
            and owned <= 256 * LANES
            and types % 8 == 0
            and types <= LANES
        )
        if fits:
            return fast_body(cells, pools_axis, fractions, order, density, area, harvest)
        return general_body(fractions, order, density, area, harvest)

    return jax.shard_map(
        body,
        mesh=mesh,
        in_specs=(P(None, "cell"), P("cell"), P("pool", None, "cell"), P(None, "cell"), P("pool")),
        out_specs=(P("pool", None, "cell"), P(None, "cell"), P("pool", None), P()),
        check_vma=False,
    )
```

profile of v0, /device:TPU:0, one launch (start us, length us, event | category | flops | bytes accessed | tf_op | source)
XLA Modules:
  0.0 33.0 jit_solution(16997924519697857931)
XLA Ops:
  0.6 1.9 %shard_map.84 = (bf16[272,128]{1,0:T(8,128)(2,1)S(1)}, bf16[272,128]{1,0:T(8,128)(2,1)S(1)}, bf16[272,128]{1,0:T(8,128)(2,1)S(1)}, bf16[272,128]{1,0:T(8,128)(2,...) custom-call(s32[1,1024]{1,0:T(1,128)} %bitcast.5, bf16[256,1024]{1,0:T(8,128)(2,1)} %refs_1_.1, ...), custom_call_target="tpu_custom_call" | custom-call | tf_op jit(solution)/shard_map/pallas_call | solution.py:156
  2.5 5.1 %collective-permute-start.2 = (bf16[272,128]{1,0:T(8,128)(2,1)S(1)}, bf16[272,128]{1,0:T(8,128)(2,1)S(1)}, u32[]{:S(2)}, u32[]{:S(2)}) collective-permute-start(bf16[272,128]{1,0:T(8,128)(2,1)S(1)} %get-tuple-element.19), channel_id=1, source_target_pairs={{0,24},{1,29},{2,26},{3,31},{4,28},{5,25},{6,30},{7,27},{8,16},{9,... | collective-permute-start | bytes 208904 | tf_op jit(solution)/shard_map/ppermute | solution.py:195
  7.6 0.0 collective-permute-start.3
  7.7 0.6 %collective-permute-start.4 = (bf16[272,128]{1,0:T(8,128)(2,1)S(1)}, bf16[272,128]{1,0:T(8,128)(2,1)S(1)}, u32[]{:S(2)}, u32[]{:S(2)}) collective-permute-start(bf16[272,128]{1,0:T(8,128)(2,1)S(1)} %get-tuple-element.21), channel_id=1, source_target_pairs={{0,8},{1,13},{2,10},{3,15},{4,12},{5,9},{6,14},{7,11},{8,0},{9,5},... | collective-permute-start | bytes 208904 | tf_op jit(solution)/shard_map/ppermute | solution.py:195
  8.3 3.6 %collective-permute-start.8 = (bf16[272,128]{1,0:T(8,128)(2,1)S(1)}, bf16[272,128]{1,0:T(8,128)(2,1)S(1)}, u32[]{:S(2)}, u32[]{:S(2)}) collective-permute-start(bf16[272,128]{1,0:T(8,128)(2,1)S(1)} %get-tuple-element.22), channel_id=1, source_target_pairs={{0,4},{2,6},{4,0},{6,2},{8,12},{10,14},{12,8},{14,10},{16,20},{18,... | collective-permute-start | bytes 208904 | tf_op jit(solution)/shard_map/ppermute | solution.py:195
  11.9 0.1 collective-permute-start
  11.9 0.0 collective-permute-done.2.refs_1_
  11.9 0.5 %collective-permute-start.5 = (bf16[272,128]{1,0:T(8,128)(2,1)S(1)}, bf16[272,128]{1,0:T(8,128)(2,1)S(1)}, u32[]{:S(2)}, u32[]{:S(2)}) collective-permute-start(bf16[272,128]{1,0:T(8,128)(2,1)S(1)} %collective-permute-done.2.refs_1_), channel_id=1, source_target_pairs={{0,1},{1,0},{2,3},{3,2},{4,5},{5,4},{6,7},{7,6},{8,9},{9,8},{10,11... | collective-permute-start | bytes 208904 | tf_op jit(solution)/shard_map/ppermute | solution.py:235
  12.4 2.0 %collective-permute-done.3.refs_2_ = bf16[272,128]{1,0:T(8,128)(2,1)S(1)} collective-permute-done((bf16[272,128]{1,0:T(8,128)(2,1)S(1)}, bf16[272,128]{1,0:T(8,128)(2,1)S(1)}, u32[]{:S(2)}, u32[]{:S(2)}) %collective-permute-start.3) | collective-permute-done | bytes 69664 | tf_op jit(solution)/shard_map/ppermute | solution.py:195
  14.4 0.0 collective-permute-start.6
  14.4 0.0 collective-permute-done.4.refs_3_
  14.4 0.5 %collective-permute-start.7 = (bf16[272,128]{1,0:T(8,128)(2,1)S(1)}, bf16[272,128]{1,0:T(8,128)(2,1)S(1)}, u32[]{:S(2)}, u32[]{:S(2)}) collective-permute-start(bf16[272,128]{1,0:T(8,128)(2,1)S(1)} %collective-permute-done.4.refs_3_), channel_id=1, source_target_pairs={{0,1},{1,0},{2,3},{3,2},{4,5},{5,4},{6,7},{7,6},{8,9},{9,8},{10,11... | collective-permute-start | bytes 208904 | tf_op jit(solution)/shard_map/ppermute | solution.py:235
  14.9 0.0 collective-permute-done.8.refs_1_
  14.9 0.1 collective-permute-start.9
  15.0 0.0 collective-permute-done
  15.0 1.6 %collective-permute-start.1 = (f32[16,1024]{1,0:T(8,128)S(1)}, f32[16,1024]{1,0:T(8,128)S(1)}, u32[]{:S(2)}, u32[]{:S(2)}) collective-permute-start(f32[16,1024]{1,0:T(8,128)S(1)} %add.9.weighted_a), channel_id=1, source_target_pairs={{0,2},{1,3},{2,0},{3,1},{4,6},{5,7},{6,4},{7,5},{8,10},{9,11},{10,... | collective-permute-start | bytes 196616 | tf_op jit(solution)/shard_map/ppermute | solution.py:235
  16.6 0.0 collective-permute-done.5.refs_4_
  16.6 0.0 collective-permute-done.6.refs_5_
  16.6 0.0 copy-start
  16.6 0.0 copy-start.1
  16.6 0.0 copy-start.2
  16.6 0.6 %shard_map.85.early_ref = bf16[256,1024]{1,0:T(8,128)(2,1)S(1)} custom-call(bf16[272,128]{1,0:T(8,128)(2,1)S(1)} %get-tuple-element.18.refs_0_, bf16[272,128]{1,0:T(8,128)(2,1)S(1)} %collective-permute-done.2.refs_1_, bf16[272,128]{1,0:T(8,128)(2,1)S(1)} %collective-permute-done.3.refs_2_, bf16[272,128]{1,0:T(8,128)(2,1)S(1)} %collective-permute-done.4.refs_3_, ...), custom_call_target="tpu_custom_call" | custom-call | flops 536870912 | bytes 524288 | tf_op jit(solution)/shard_map/pallas_call | solution.py:156
  17.2 2.3 %collective-permute-done.1.weighted_b = f32[16,1024]{1,0:T(8,128)S(1)} collective-permute-done((f32[16,1024]{1,0:T(8,128)S(1)}, f32[16,1024]{1,0:T(8,128)S(1)}, u32[]{:S(2)}, u32[]{:S(2)}) %collective-permute-start.1) | collective-permute-done | bytes 65568 | tf_op jit(solution)/shard_map/ppermute | solution.py:235
  19.5 0.0 collective-permute-done.7.refs_0_
  19.5 0.0 collective-permute-done.9.refs_2_
  19.5 0.0 copy-done
  19.5 0.0 copy-done.1
  19.5 0.0 copy-done.2
  19.6 1.1 %shard_map.86 = (f32[2,16,1024]{2,1,0:T(8,128)S(1)}, f32[16,1024]{1,0:T(8,128)S(1)}, f32[8,128]{1,0:T(8,128)S(1)}) custom-call(f32[1,2]{1,0:T(1,128)S(1)} %bitcast.4, f32[2,16,1024]{2,1,0:T(8,128)S(1)} %copy-done, f32[16,1024]{1,0:T(8,128)S(1)} %copy-done.1, f32[16,1024]{1,0:T(8,128)S(1)} %add.9.weighted_a, ...), custom_call_target="tpu_custom_call" | custom-call | tf_op jit(solution)/shard_map/pallas_call | solution.py:156
  20.7 1.4 %collective-permute-start.10 = (f32[8,128]{1,0:T(8,128)S(1)}, f32[8,128]{1,0:T(8,128)S(1)}, u32[]{:S(2)}, u32[]{:S(2)}) collective-permute-start(f32[8,128]{1,0:T(8,128)S(1)} %get-tuple-element.27), channel_id=1, source_target_pairs={{0,4},{4,0},{8,12},{12,8},{16,20},{20,16},{24,28},{28,24},{1,5},{5... | collective-permute-start | bytes 12296 | tf_op jit(solution)/shard_map/ppermute | solution.py:235
  22.0 2.2 %collective-permute-done.10 = f32[8,128]{1,0:T(8,128)S(1)} collective-permute-done((f32[8,128]{1,0:T(8,128)S(1)}, f32[8,128]{1,0:T(8,128)S(1)}, u32[]{:S(2)}, u32[]{:S(2)}) %collective-permute-start.10) | collective-permute-done | bytes 4128 | tf_op jit(solution)/shard_map/ppermute | solution.py:235
  24.3 0.9 %collective-permute-start.11 = (f32[8,128]{1,0:T(8,128)S(1)}, f32[8,128]{1,0:T(8,128)S(1)}, u32[]{:S(2)}, u32[]{:S(2)}) collective-permute-start(f32[8,128]{1,0:T(8,128)S(1)} %add.10), channel_id=1, source_target_pairs={{0,8},{4,12},{8,0},{12,4},{16,24},{20,28},{24,16},{28,20},{1,9},{5... | collective-permute-start | bytes 12296 | tf_op jit(solution)/shard_map/ppermute | solution.py:235
  25.2 2.7 %collective-permute-done.11 = f32[8,128]{1,0:T(8,128)S(1)} collective-permute-done((f32[8,128]{1,0:T(8,128)S(1)}, f32[8,128]{1,0:T(8,128)S(1)}, u32[]{:S(2)}, u32[]{:S(2)}) %collective-permute-start.11) | collective-permute-done | bytes 4128 | tf_op jit(solution)/shard_map/ppermute | solution.py:235
  27.9 1.8 %collective-permute-start.12 = (f32[8,128]{1,0:T(8,128)S(1)}, f32[8,128]{1,0:T(8,128)S(1)}, u32[]{:S(2)}, u32[]{:S(2)}) collective-permute-start(f32[8,128]{1,0:T(8,128)S(1)} %add.11.sums_a), channel_id=1, source_target_pairs={{0,16},{4,20},{8,24},{12,28},{16,0},{20,4},{24,8},{28,12},{1,17},{... | collective-permute-start | bytes 12296 | tf_op jit(solution)/shard_map/ppermute | solution.py:235
  29.7 0.7 %shard_map.87 = (f32[2,16,1024]{2,1,0:T(8,128)}, f32[16,1024]{1,0:T(8,128)}) custom-call(f32[2,16,1024]{2,1,0:T(8,128)S(1)} %get-tuple-element.23.stock_ref, f32[16,1024]{1,0:T(8,128)S(1)} %get-tuple-element.24.area_ref), custom_call_target="tpu_custom_call" | custom-call | tf_op jit(solution)/shard_map/pallas_call | solution.py:156
  30.4 2.0 %collective-permute-done.12.sums_b = f32[8,128]{1,0:T(8,128)S(1)} collective-permute-done((f32[8,128]{1,0:T(8,128)S(1)}, f32[8,128]{1,0:T(8,128)S(1)}, u32[]{:S(2)}, u32[]{:S(2)}) %collective-permute-start.12) | collective-permute-done | bytes 4128 | tf_op jit(solution)/shard_map/ppermute | solution.py:235
  32.4 0.6 %shard_map.88 = (f32[2,16]{1,0:T(2,128)}, f32[1,16]{1,0:T(1,128)}) custom-call(f32[8,128]{1,0:T(8,128)S(1)} %add.11.sums_a, f32[8,128]{1,0:T(8,128)S(1)} %collective-permute-done.12.sums_b), custom_call_target="tpu_custom_call" | custom-call | tf_op jit(solution)/shard_map/pallas_call | solution.py:156
  (3 shorter events, 0.0 us)
Async XLA Ops:
  2.5 9.4 %collective-permute-start.2 = (bf16[272,128]{1,0:T(8,128)(2,1)S(1)}, bf16[272,128]{1,0:T(8,128)(2,1)S(1)}, u32[]{:S(2)}, u32[]{:S(2)}) collective-permute-start(bf16[272,128]{1,0:T(8,128)(2,1)S(1)} %get-tuple-element.19), channel_id=1, source_target_pairs={{0,24},{1,29},{2,26},{3,31},{4,28},{5,25},{6,30},{7,27},{8,16},{9,... | collective-permute-start | bytes 208904 | tf_op jit(solution)/shard_map/ppermute | solution.py:195
  7.6 6.8 %collective-permute-start.3 = (bf16[272,128]{1,0:T(8,128)(2,1)S(1)}, bf16[272,128]{1,0:T(8,128)(2,1)S(1)}, u32[]{:S(2)}, u32[]{:S(2)}) collective-permute-start(bf16[272,128]{1,0:T(8,128)(2,1)S(1)} %get-tuple-element.20), channel_id=1, source_target_pairs={{0,16},{1,21},{2,18},{3,23},{4,20},{5,17},{6,22},{7,19},{8,24},{9,... | collective-permute-start | bytes 208904 | tf_op jit(solution)/shard_map/ppermute | solution.py:195
  7.7 6.8 %collective-permute-start.4 = (bf16[272,128]{1,0:T(8,128)(2,1)S(1)}, bf16[272,128]{1,0:T(8,128)(2,1)S(1)}, u32[]{:S(2)}, u32[]{:S(2)}) collective-permute-start(bf16[272,128]{1,0:T(8,128)(2,1)S(1)} %get-tuple-element.21), channel_id=1, source_target_pairs={{0,8},{1,13},{2,10},{3,15},{4,12},{5,9},{6,14},{7,11},{8,0},{9,5},... | collective-permute-start | bytes 208904 | tf_op jit(solution)/shard_map/ppermute | solution.py:195
  8.3 6.6 %collective-permute-start.8 = (bf16[272,128]{1,0:T(8,128)(2,1)S(1)}, bf16[272,128]{1,0:T(8,128)(2,1)S(1)}, u32[]{:S(2)}, u32[]{:S(2)}) collective-permute-start(bf16[272,128]{1,0:T(8,128)(2,1)S(1)} %get-tuple-element.22), channel_id=1, source_target_pairs={{0,4},{2,6},{4,0},{6,2},{8,12},{10,14},{12,8},{14,10},{16,20},{18,... | collective-permute-start | bytes 208904 | tf_op jit(solution)/shard_map/ppermute | solution.py:195
  11.9 3.1 %collective-permute-start = (f32[16,1024]{1,0:T(8,128)S(1)}, f32[16,1024]{1,0:T(8,128)S(1)}, u32[]{:S(2)}, u32[]{:S(2)}) collective-permute-start(f32[16,1024]{1,0:T(8,128)S(1)} %get-tuple-element.17), channel_id=1, source_target_pairs={{0,1},{1,0},{2,3},{3,2},{4,5},{5,4},{6,7},{7,6},{8,9},{9,8},{10,11... | collective-permute-start | bytes 196616 | tf_op jit(solution)/shard_map/ppermute | solution.py:235
  11.9 4.6 %collective-permute-start.5 = (bf16[272,128]{1,0:T(8,128)(2,1)S(1)}, bf16[272,128]{1,0:T(8,128)(2,1)S(1)}, u32[]{:S(2)}, u32[]{:S(2)}) collective-permute-start(bf16[272,128]{1,0:T(8,128)(2,1)S(1)} %collective-permute-done.2.refs_1_), channel_id=1, source_target_pairs={{0,1},{1,0},{2,3},{3,2},{4,5},{5,4},{6,7},{7,6},{8,9},{9,8},{10,11... | collective-permute-start | bytes 208904 | tf_op jit(solution)/shard_map/ppermute | solution.py:235
  14.4 2.2 %collective-permute-start.6 = (bf16[272,128]{1,0:T(8,128)(2,1)S(1)}, bf16[272,128]{1,0:T(8,128)(2,1)S(1)}, u32[]{:S(2)}, u32[]{:S(2)}) collective-permute-start(bf16[272,128]{1,0:T(8,128)(2,1)S(1)} %collective-permute-done.3.refs_2_), channel_id=1, source_target_pairs={{0,1},{1,0},{2,3},{3,2},{4,5},{5,4},{6,7},{7,6},{8,9},{9,8},{10,11... | collective-permute-start | bytes 208904 | tf_op jit(solution)/shard_map/ppermute | solution.py:235
  14.4 5.1 %collective-permute-start.7 = (bf16[272,128]{1,0:T(8,128)(2,1)S(1)}, bf16[272,128]{1,0:T(8,128)(2,1)S(1)}, u32[]{:S(2)}, u32[]{:S(2)}) collective-permute-start(bf16[272,128]{1,0:T(8,128)(2,1)S(1)} %collective-permute-done.4.refs_3_), channel_id=1, source_target_pairs={{0,1},{1,0},{2,3},{3,2},{4,5},{5,4},{6,7},{7,6},{8,9},{9,8},{10,11... | collective-permute-start | bytes 208904 | tf_op jit(solution)/shard_map/ppermute | solution.py:235
  14.9 4.6 %collective-permute-start.9 = (bf16[272,128]{1,0:T(8,128)(2,1)S(1)}, bf16[272,128]{1,0:T(8,128)(2,1)S(1)}, u32[]{:S(2)}, u32[]{:S(2)}) collective-permute-start(bf16[272,128]{1,0:T(8,128)(2,1)S(1)} %collective-permute-done.8.refs_1_), channel_id=1, source_target_pairs={{0,1},{1,0},{2,3},{3,2},{4,5},{5,4},{6,7},{7,6},{8,9},{9,8},{10,11... | collective-permute-start | bytes 208904 | tf_op jit(solution)/shard_map/ppermute | solution.py:235
  15.0 4.5 %collective-permute-start.1 = (f32[16,1024]{1,0:T(8,128)S(1)}, f32[16,1024]{1,0:T(8,128)S(1)}, u32[]{:S(2)}, u32[]{:S(2)}) collective-permute-start(f32[16,1024]{1,0:T(8,128)S(1)} %add.9.weighted_a), channel_id=1, source_target_pairs={{0,2},{1,3},{2,0},{3,1},{4,6},{5,7},{6,4},{7,5},{8,10},{9,11},{10,... | collective-permute-start | bytes 196616 | tf_op jit(solution)/shard_map/ppermute | solution.py:235
  16.6 2.9 %copy-start = (f32[2,16,1024]{2,1,0:T(8,128)S(1)}, f32[2,16,1024]{2,1,0:T(8,128)}, u32[]{:S(2)}) copy-start(f32[2,16,1024]{2,1,0:T(8,128)} %density_ref.1) | copy-start | bytes 393220
  16.6 2.9 %copy-start.1 = (f32[16,1024]{1,0:T(8,128)S(1)}, f32[16,1024]{1,0:T(8,128)}, u32[]{:S(2)}) copy-start(f32[16,1024]{1,0:T(8,128)} %area_ref.1) | copy-start | bytes 196612
  16.6 2.9 %copy-start.2 = (f32[2]{0:T(128)S(1)}, f32[2]{0:T(128)}, u32[]{:S(2)}) copy-start(f32[2]{0:T(128)} %param.9) | copy-start | bytes 28
  20.7 3.6 %collective-permute-start.10 = (f32[8,128]{1,0:T(8,128)S(1)}, f32[8,128]{1,0:T(8,128)S(1)}, u32[]{:S(2)}, u32[]{:S(2)}) collective-permute-start(f32[8,128]{1,0:T(8,128)S(1)} %get-tuple-element.27), channel_id=1, source_target_pairs={{0,4},{4,0},{8,12},{12,8},{16,20},{20,16},{24,28},{28,24},{1,5},{5... | collective-permute-start | bytes 12296 | tf_op jit(solution)/shard_map/ppermute | solution.py:235
  24.3 3.6 %collective-permute-start.11 = (f32[8,128]{1,0:T(8,128)S(1)}, f32[8,128]{1,0:T(8,128)S(1)}, u32[]{:S(2)}, u32[]{:S(2)}) collective-permute-start(f32[8,128]{1,0:T(8,128)S(1)} %add.10), channel_id=1, source_target_pairs={{0,8},{4,12},{8,0},{12,4},{16,24},{20,28},{24,16},{28,20},{1,9},{5... | collective-permute-start | bytes 12296 | tf_op jit(solution)/shard_map/ppermute | solution.py:235
  27.9 4.5 %collective-permute-start.12 = (f32[8,128]{1,0:T(8,128)S(1)}, f32[8,128]{1,0:T(8,128)S(1)}, u32[]{:S(2)}, u32[]{:S(2)}) collective-permute-start(f32[8,128]{1,0:T(8,128)S(1)} %add.11.sums_a), channel_id=1, source_target_pairs={{0,16},{4,20},{8,24},{12,28},{16,0},{20,4},{24,8},{28,12},{1,17},{... | collective-permute-start | bytes 12296 | tf_op jit(solution)/shard_map/ppermute | solution.py:235
where the time goes:
time: 33.2 us; the launch traced here: 33 us
  starting transfers between devices  16.2 us (49%)
  waiting for transfers between devices  11.2 us (34%)
  Pallas kernels  4.86 us (15%)
  between operations  0.73 us (2%)
    ppermute x4, starting transfers between devices, fast_body(): received.append(lax.ppermute(packed[1 + k], ('cell', 'pool'), pairs))  9.35 us
    ppermute x9, waiting for transfers between devices, swap(): return lax.ppermute(value, axis, [(n, n ^ step) for n in range(size)])  9.2 us
    ppermute x9, starting transfers between devices, swap(): return lax.ppermute(value, axis, [(n, n ^ step) for n in range(size)])  6.83 us
    pallas_call x5, Pallas kernels, call(): pl.pallas_call(kernel, out_shape=out_shape, in_specs=[pl.BlockSpec(memory...  4.86 us
    ppermute x4, waiting for transfers between devices, fast_body(): received.append(lax.ppermute(packed[1 + k], ('cell', 'pool'), pairs))  1.98 us
  transfers between devices with their start and end apart: 13, of which 5 were waited for; matrix products, arithmetic and copies ran while one was open for 0% of the time, Pallas kernels for 4%

commit v1 on v0

--- a/solution.py
+++ b/solution.py
@@ -22,7 +22,8 @@
 
 def pack_kernel(*refs, even, odd):
     count = 1 + len(even)
-    sources, (*out_refs, weighted_out), loaded, arrived = refs[:5], refs[5:6 + count], refs[6 + count:-1], refs[-1]
+    sources, (*out_refs, weighted_out, split_out, harvest_out) = refs[:5], refs[5:8 + count]
+    loaded, arrived = refs[8 + count:-1], refs[-1]
     order_vmem, frac, harvest, density, area = loaded
     copies = [
         pltpu.make_async_copy(source, target, arrived.at[n])
@@ -37,7 +38,7 @@
     core = lax.rem(lax.axis_index("pool"), 2)
     want = jnp.where(iota((rows, LANES), 0) == 0, cell, -1)
     for k, a in enumerate(even):
-        target = cell ^ jnp.where(core == 0, a, odd[k] if k < len(odd) else 0)
+        target = cell ^ jnp.where(core == 0, a, odd[k])
         want = jnp.where(iota((rows, LANES), 0) == k + 1, target, want)
     sums = jnp.where(iota((LANES, 2 * LANES), 0) < iota((LANES, 2 * LANES), 1), 1.0, 0.0).astype(BF16)
     copies[0].wait()
@@ -63,7 +64,10 @@
     for copy in copies[2:]:
         copy.wait()
     pools = density.shape[0]
-    weighted_out[...] = area[...] * sum(harvest[:, p:p + 1] * density[p] for p in range(pools))
+    stock = [area[...] * density[p] for p in range(pools)]
+    weighted_out[...] = sum(harvest[:, p:p + 1] * stock[p] for p in range(pools))
+    harvest_out[...] = harvest[...]
+    split_out[...] = in_parts(jnp.concatenate(stock, axis=0))
     copies[1].wait()
     data = jnp.concatenate([frac[...], extra], axis=0)
     packed = lax.dot_general(data, onehot, NT, preferred_element_type=F32).astype(BF16)
@@ -71,82 +75,113 @@
         out_refs[k][...] = packed[:, k * width:(k + 1) * width]
 
 
+def in_parts(values):
+    parts = []
+    for _ in range(3):
+        parts.append(values.astype(BF16))
+        values = values - parts[-1].astype(F32)
+    return jnp.concatenate(parts, axis=0)
+
+
 def matches(row, height):
     steps = iota((height, row.shape[1]), 0).astype(F32).astype(BF16)
     one = jnp.ones(steps.shape, BF16)
     return jnp.where(steps == row.astype(BF16), one, jnp.zeros_like(one))
 
 
-def placed(parts, kinds, owned):
+def arrived_columns(refs, kinds, owned):
+    parts = [ref[...] for ref in refs]
     data = jnp.concatenate(parts, axis=1)
     tail = data[kinds:].astype(F32)
     high, low = tail[0:1], tail[1:2]
-    onehot = jnp.concatenate(
-        [matches(jnp.where(high == b, low, -1.0), LANES) for b in range(owned // LANES)], axis=0
-    )
-    return lax.dot_general(data[:kinds], onehot, NT, preferred_element_type=F32)
-
-
-def place_kernel(*refs):
-    kinds, owned = refs[-1].shape
-    refs[-1][...] = placed([ref[...] for ref in refs[:-1]], kinds, owned).astype(BF16)
-
-
-def transition_kernel(harvest_ref, density_ref, area_ref, weighted_a, weighted_b, early_ref, *refs, parts):
-    stock_out, area_out, sums_out, block = refs[parts:]
+    onehot = [matches(jnp.where(high == b, low, -1.0), LANES) for b in range(owned // LANES)]
+    return data[:kinds], jnp.concatenate(onehot, axis=0)
+
+
+def place_kernel(split_ref, *refs):
+    *chunk_refs, placed_out, gram_out = refs
+    data, onehot = arrived_columns(chunk_refs, *placed_out.shape)
+    placed = lax.dot_general(data, onehot, NT, preferred_element_type=F32).astype(BF16)
+    placed_out[...] = placed
+    gram_out[...] = lax.dot_general(placed, split_ref[...], NT, preferred_element_type=F32)
+
+
+def per_type(gram, types):
+    gram = gram.reshape(types, types, gram.shape[1])
+    own = iota(gram.shape, 1) == lax.rem(iota(gram.shape, 2), types)
+    return jnp.sum(jnp.where(own, gram, 0.0), axis=1)
+
+
+def sums_kernel(harvest_ref, weighted_a, weighted_b, split_ref, placed_ref, gram_ref, *refs):
+    *chunk_refs, sums_out = refs
+    kinds, owned = placed_ref.shape
+    types = weighted_a.shape[0]
+    pools = split_ref.shape[0] // (3 * types)
+    data, onehot = arrived_columns(chunk_refs, kinds, owned)
+    split = split_ref[...]
+    weighted = in_parts(weighted_a[...] + weighted_b[...])
+    late = lax.dot_general(jnp.concatenate([split, weighted], axis=0), onehot, NN, preferred_element_type=F32).astype(BF16)
+    edge = split.shape[0]
+    gram = gram_ref[...] + lax.dot_general(data, late[:edge], NT, preferred_element_type=F32)
+    gram_weighted = lax.dot_general(placed_ref[...], weighted, NT, preferred_element_type=F32)
+    gram_weighted = gram_weighted + lax.dot_general(data, late[edge:], NT, preferred_element_type=F32)
+    rows = []
+    diagonal = iota((types, LANES), 0) == iota((types, LANES), 1)
+    by_lane = per_type(gram, types)
+    lane = iota(by_lane.shape, 1)
+    same = lax.rem(lane, types) == iota(by_lane.shape, 0)
+    for p in range(pools):
+        mine = lax.rem(lax.div(lane, types), pools) == p
+        scale = jnp.where(same, 1.0, 1.0 - harvest_ref[:, p:p + 1])
+        rows.append(jnp.sum(jnp.where(mine, by_lane * scale, 0.0), axis=1, keepdims=True))
+    by_lane = per_type(gram_weighted, types)
+    same = lax.rem(iota(by_lane.shape, 1), types) == iota(by_lane.shape, 0)
+    rows.append(jnp.sum(jnp.where(same, 0.0, by_lane), axis=1, keepdims=True))
+    rows = [jnp.sum(jnp.where(diagonal, r, 0.0), axis=0, keepdims=True) for r in rows]
+    rows.append(jnp.zeros((sums_out.shape[0] - len(rows), LANES), F32))
+    sums_out[...] = jnp.concatenate(rows, axis=0)
+
+
+def density_kernel(harvest_ref, density_ref, area_ref, placed_ref, *refs):
+    *chunk_refs, density_out, cum_out, block = refs
     pools, types, owned = density_ref.shape
     kinds = types * types
     blocks = owned // LANES
-    last = [ref[...] for ref in refs[:parts]]
-    late = placed(last[:-2] + [last[-2] + last[-1]], kinds, owned) + early_ref[...].astype(F32)
+    data, onehot = arrived_columns(chunk_refs, kinds, owned)
+    late = lax.dot_general(data, onehot, NT, preferred_element_type=F32) + placed_ref[...].astype(F32)
     for b in range(blocks):
         block[b * kinds:(b + 1) * kinds] = late[:, b * LANES:(b + 1) * LANES]
     dest = iota((types, LANES), 0)
-    sums = [jnp.zeros((types, LANES), F32) for _ in range(pools + 1)]
     for b in range(blocks):
         at = slice(b * LANES, (b + 1) * LANES)
         area = area_ref[:, at]
         stock = [area * density_ref[p, :, at] for p in range(pools)]
-        sources = stock + [weighted_a[:, at] + weighted_b[:, at], area]
+        sources = stock + [area]
         totals = [jnp.zeros((types, LANES), F32) for _ in sources]
         staying = jnp.zeros((types, LANES), F32)
         for j in range(types):
             column = block[pl.ds(b * kinds + j, types, stride=types), :]
             staying = jnp.where(dest == j, column, staying)
             totals = [t + column * s[j:j + 1] for t, s in zip(totals, sources)]
+        running = totals[-1]
+        inverse = 1.0 / running
         for p in range(pools):
             kept = staying * stock[p]
-            new_stock = kept + (1.0 - harvest_ref[:, p:p + 1]) * (totals[p] - kept)
-            stock_out[p, :, at] = new_stock
-            sums[p] = sums[p] + new_stock
-        sums[pools] = sums[pools] + (totals[pools] - staying * sources[pools])
-        area_out[:, at] = totals[-1]
-    diagonal = dest == iota((types, LANES), 1)
-    rows = []
-    for s in sums:
-        each = jnp.sum(s, axis=1, keepdims=True)
-        rows.append(jnp.sum(jnp.where(diagonal, each, 0.0), axis=0, keepdims=True))
-    rows.append(jnp.zeros((sums_out.shape[0] - len(rows), LANES), F32))
-    sums_out[...] = jnp.concatenate(rows, axis=0)
-
-
-def density_kernel(stock_ref, area_ref, density_out, cum_out):
-    pools, types, owned = stock_ref.shape
-    running = area_ref[...]
-    inverse = 1.0 / running
-    for p in range(pools):
-        density_out[p] = stock_ref[p] * inverse
-    dest = iota((types, owned), 0)
-    step = 1
-    while step < types:
-        running = running + jnp.where(dest >= step, pltpu.roll(running, step, 0), 0.0)
-        step *= 2
-    cum_out[...] = running / running[types - 1:types]
-
-
-def finish_kernel(sums_a, sums_b, mean_out, removed_out, *, scale):
+            density_out[p, :, at] = (kept + (1.0 - harvest_ref[:, p:p + 1]) * (totals[p] - kept)) * inverse
+        step = 1
+        while step < types:
+            running = running + jnp.where(dest >= step, pltpu.roll(running, step, 0), 0.0)
+            step *= 2
+        cum_out[:, at] = running / running[types - 1:types]
+
+
+def finish_kernel(*refs, scale):
+    *sums_refs, mean_out, removed_out = refs
     pools, types = mean_out.shape
-    sums = (sums_a[...] + sums_b[...]) * scale
+    level = [ref[...] for ref in sums_refs]
+    while len(level) > 1:
+        level = [a + b for a, b in zip(level[0::2], level[1::2])]
+    sums = level[0] * scale
     mean_out[...] = sums[:pools, :types]
     removed_out[...] = sums[pools:pools + 1, :types]
 
@@ -176,57 +211,46 @@
     count = 1 + len(even)
     harvest = harvest.reshape(1, pools)
     sources = (order.reshape(1, owned), fractions, harvest, density, area)
-    *packed, weighted = call(
+    *packed, weighted, split, harvest = call(
         functools.partial(pack_kernel, even=even, odd=odd),
-        [array(kinds + 16, chunk, dtype=BF16)] * count + [array(types, owned)],
+        [array(kinds + 16, chunk, dtype=BF16)] * count
+        + [array(types, owned), array(3 * pools * types, owned, dtype=BF16), array(1, pools)],
         [pltpu.with_memory_space_constraint(x, pltpu.HBM) for x in sources],
         scratch=[pltpu.VMEM(x.shape, x.dtype) for x in sources] + [pltpu.SemaphoreType.DMA((len(sources),))],
         space=pltpu.HBM,
     )
-    received = []
-    for k, a in enumerate(even):
-        b = odd[k] if k < len(odd) else None
-        pairs = []
-        for c in range(cells):
-            for p in range(pools_axis):
-                s = a if p % 2 == 0 else b
-                if s is not None:
-                    pairs.append((c * pools_axis + p, (c ^ s) * pools_axis + p))
+    received, other = [], []
+    for k, hops in enumerate(zip(even, odd)):
+        pairs = [
+            (c * pools_axis + p, (c ^ hops[p % 2]) * pools_axis + p) for c in range(cells) for p in range(pools_axis)
+        ]
         received.append(lax.ppermute(packed[1 + k], ("cell", "pool"), pairs))
-    other = []
-    for r in received:
-        other.append(swap(r, "pool", pools_axis, 1))
+        if hops[0] != hops[1]:
+            other.append(swap(received[k], "pool", pools_axis, 1))
     step = 1
     while step < pools_axis // 2:
         weighted = weighted + swap(weighted, "pool", pools_axis, step)
         step *= 2
     weighted_far = swap(weighted, "pool", pools_axis, step)
-    early = [packed[0]] + received[:-1] + other[:-2]
-    placed_early = call(
-        place_kernel,
-        array(kinds, owned, dtype=BF16),
-        early,
-        cost=pl.CostEstimate(flops=2 * kinds * owned * owned, bytes_accessed=2 * kinds * owned, transcendentals=0),
-    )
-    late = [other[-2], received[-1], other[-1]]
-    new_stock, new_area, sums = call(
-        functools.partial(transition_kernel, parts=len(late)),
-        [array(pools, types, owned), array(types, owned), array(8, LANES)],
-        (harvest, density, area, weighted, weighted_far, placed_early, *late),
+    early = [packed[0]] + received[:-1] + other[:EARLY]
+    placed, gram = call(place_kernel, [array(kinds, owned, dtype=BF16), array(kinds, split.shape[0])], (split, *early))
+    late = other[EARLY:] + received[-1:]
+    sums = call(sums_kernel, array(8, LANES), (harvest, weighted, weighted_far, split, placed, gram, *late))
+    new_density, area_cum = call(
+        density_kernel,
+        [array(pools, types, owned), array(types, owned)],
+        (harvest, density, area, placed, *late),
         scratch=[pltpu.VMEM((kinds * (owned // LANES), LANES), F32)],
     )
-    new_density, area_cum = call(
-        density_kernel, [array(pools, types, owned), array(types, owned)], (new_stock, new_area)
-    )
-    step = 1
-    while step < cells // 2:
+    step = cells // 2
+    while step > 2:
         sums = sums + swap(sums, "cell", cells, step)
-        step *= 2
-    last = swap(sums, "cell", cells, step)
+        step //= 2
+    group = [sums]
+    for n in range(1, min(4, cells)):
+        group.append(swap(sums, "cell", cells, n))
     mean, removed = call(
-        functools.partial(finish_kernel, scale=1.0 / (cells * owned)),
-        [array(pools, types), array(1, types)],
-        (sums, last),
+        functools.partial(finish_kernel, scale=1.0 / (cells * owned)), [array(pools, types), array(1, types)], group
     )
     return new_density, area_cum, mean, removed.reshape(types)
 
@@ -235,7 +259,8 @@
     return lax.ppermute(value, axis, [(n, n ^ step) for n in range(size)])
 
 
-SPLIT = {8: ((6, 4, 2, 1), (7, 5, 3))}
+SPLIT = {8: ((6, 2, 4, 1), (5, 7, 3, 1))}
+EARLY = 1
 
 
 def place_columns(received, positions, owned):
@@ -286,7 +311,7 @@
             and owned % (cells * LANES) == 0
             and owned <= 256 * LANES
             and types % 8 == 0
-            and types <= LANES
+            and 3 * density.shape[0] * types <= LANES
         )
         if fits:
             return fast_body(cells, pools_axis, fractions, order, density, area, harvest)

time: 33.2 us -> 31.6 us (0.952)
  waiting for transfers between devices: 11.2 us -> 9.31 us
  Pallas kernels: 4.86 us -> 5.74 us
  starting transfers between devices: 16.2 us -> 15.6 us
    ppermute x9, waiting for transfers between devices: 9.2 us -> 5.54 us  [swap(): return lax.ppermute(value, axis, [(n, n ^ step) for n in range(size)])]
    ppermute x4, starting transfers between devices: 9.35 us -> 7.45 us  [fast_body(): received.append(lax.ppermute(packed[1 + k], ('cell', 'pool'), pairs))]
    ppermute x4, waiting for transfers between devices: 1.98 us -> 3.77 us  [fast_body(): received.append(lax.ppermute(packed[1 + k], ('cell', 'pool'), pairs))]
    ppermute x9, starting transfers between devices: 6.83 us -> 8.19 us  [swap(): return lax.ppermute(value, axis, [(n, n ^ step) for n in range(size)])]
    pallas_call x5, Pallas kernels: 4.86 us -> 5.74 us  [call(): pl.pallas_call(kernel, out_shape=out_shape, in_specs=[pl.BlockSpec(memory...]
  transfers between devices with their start and end apart: 13 -> 13, of which waited for: 5 -> 5; matrix products, arithmetic and copies ran while one was open for 0% -> 0% of each run, Pallas kernels for 4% -> 8%
where the time goes in v1:
time: 31.6 us; the launch traced here: 31.4 us
  starting transfers between devices  15.6 us (49%)
  waiting for transfers between devices  9.31 us (29%)
  Pallas kernels  5.74 us (18%)
  between operations  0.69 us (2%)
    ppermute x9, starting transfers between devices, swap(): return lax.ppermute(value, axis, [(n, n ^ step) for n in range(size)])  8.19 us
    ppermute x4, starting transfers between devices, fast_body(): received.append(lax.ppermute(packed[1 + k], ('cell', 'pool'), pairs))  7.45 us
    pallas_call x5, Pallas kernels, call(): pl.pallas_call(kernel, out_shape=out_shape, in_specs=[pl.BlockSpec(memory...  5.74 us
    ppermute x9, waiting for transfers between devices, swap(): return lax.ppermute(value, axis, [(n, n ^ step) for n in range(size)])  5.54 us
    ppermute x4, waiting for transfers between devices, fast_body(): received.append(lax.ppermute(packed[1 + k], ('cell', 'pool'), pairs))  3.77 us
  transfers between devices with their start and end apart: 13, of which 5 were waited for; matrix products, arithmetic and copies ran while one was open for 0% of the time, Pallas kernels for 8%

profile of v1, /device:TPU:0, one launch (start us, length us, event | category | flops | bytes accessed | tf_op | source)
XLA Modules:
  0.0 31.4 jit_solution(6226198088150573972)
XLA Ops:
  0.6 1.9 %shard_map.84 = (bf16[272,128]{1,0:T(8,128)(2,1)S(1)}, bf16[272,128]{1,0:T(8,128)(2,1)S(1)}, bf16[272,128]{1,0:T(8,128)(2,1)S(1)}, bf16[272,128]{1,0:T(8,128)(2,...) custom-call(s32[1,1024]{1,0:T(1,128)} %bitcast.3, ...), custom_call_target="tpu_custom_call" | custom-call | tf_op jit(solution)/shard_map/pallas_call | solution.py:191
  2.5 5.1 %collective-permute-start = (bf16[272,128]{1,0:T(8,128)(2,1)S(1)}, bf16[272,128]{1,0:T(8,128)(2,1)S(1)}, u32[]{:S(2)}, u32[]{:S(2)}) collective-permute-start(bf16[272,128]{1,0:T(8,128)(2,1)S(1)} %get-tuple-element.21), channel_id=1, source_target_pairs={{0,24},{1,21},{2,26},{3,23},{4,28},{5,17},{6,30},{7,19},{8,16},{9,... | collective-permute-start | bytes 208904 | tf_op jit(solution)/shard_map/ppermute | solution.py:227
  7.7 0.0 collective-permute-start.1
  7.7 0.6 %collective-permute-start.2 = (bf16[272,128]{1,0:T(8,128)(2,1)S(1)}, bf16[272,128]{1,0:T(8,128)(2,1)S(1)}, u32[]{:S(2)}, u32[]{:S(2)}) collective-permute-start(bf16[272,128]{1,0:T(8,128)(2,1)S(1)} %get-tuple-element.23), channel_id=1, source_target_pairs={{0,16},{1,13},{2,18},{3,15},{4,20},{5,9},{6,22},{7,11},{8,24},{9,5... | collective-permute-start | bytes 208904 | tf_op jit(solution)/shard_map/ppermute | solution.py:227
  8.3 0.1 collective-permute-start.7
  8.4 2.2 %collective-permute-done.refs_1_ = bf16[272,128]{1,0:T(8,128)(2,1)S(1)} collective-permute-done((bf16[272,128]{1,0:T(8,128)(2,1)S(1)}, bf16[272,128]{1,0:T(8,128)(2,1)S(1)}, u32[]{:S(2)}, u32[]{:S(2)}) %collective-permute-start) | collective-permute-done | bytes 69664 | tf_op jit(solution)/shard_map/ppermute | solution.py:227
  10.6 0.0 collective-permute-start.3
  10.6 1.7 %collective-permute-start.6 = (bf16[272,128]{1,0:T(8,128)(2,1)S(1)}, bf16[272,128]{1,0:T(8,128)(2,1)S(1)}, u32[]{:S(2)}, u32[]{:S(2)}) collective-permute-start(bf16[272,128]{1,0:T(8,128)(2,1)S(1)} %get-tuple-element.25), channel_id=1, source_target_pairs={{0,4},{1,5},{2,6},{3,7},{4,0},{5,1},{6,2},{7,3},{8,12},{9,13},{10,... | collective-permute-start | bytes 208904 | tf_op jit(solution)/shard_map/ppermute | solution.py:227
  12.3 1.5 %collective-permute-done.1.refs_2_ = bf16[272,128]{1,0:T(8,128)(2,1)S(1)} collective-permute-done((bf16[272,128]{1,0:T(8,128)(2,1)S(1)}, bf16[272,128]{1,0:T(8,128)(2,1)S(1)}, u32[]{:S(2)}, u32[]{:S(2)}) %collective-permute-start.1) | collective-permute-done | bytes 69664 | tf_op jit(solution)/shard_map/ppermute | solution.py:227
  13.8 0.0 collective-permute-start.4
  13.8 0.0 collective-permute-done.2.refs_3_
  13.8 0.5 %collective-permute-start.5 = (bf16[272,128]{1,0:T(8,128)(2,1)S(1)}, bf16[272,128]{1,0:T(8,128)(2,1)S(1)}, u32[]{:S(2)}, u32[]{:S(2)}) collective-permute-start(bf16[272,128]{1,0:T(8,128)(2,1)S(1)} %collective-permute-done.2.refs_3_), channel_id=1, source_target_pairs={{0,1},{1,0},{2,3},{3,2},{4,5},{5,4},{6,7},{7,6},{8,9},{9,8},{10,11... | collective-permute-start | bytes 208904 | tf_op jit(solution)/shard_map/ppermute | solution.py:259
  14.3 0.0 collective-permute-done.7
  14.4 1.5 %collective-permute-start.8 = (f32[16,1024]{1,0:T(8,128)S(1)}, f32[16,1024]{1,0:T(8,128)S(1)}, u32[]{:S(2)}, u32[]{:S(2)}) collective-permute-start(f32[16,1024]{1,0:T(8,128)S(1)} %add.6.weighted_a), channel_id=1, source_target_pairs={{0,2},{1,3},{2,0},{3,1},{4,6},{5,7},{6,4},{7,5},{8,10},{9,11},{10,... | collective-permute-start | bytes 196616 | tf_op jit(solution)/shard_map/ppermute | solution.py:259
  15.9 0.0 collective-permute-done.3.refs_4_
  15.9 0.9 %shard_map.85 = (bf16[256,1024]{1,0:T(8,128)(2,1)S(1)}, f32[256,96]{1,0:T(8,128)S(1)}) custom-call(bf16[96,1024]{1,0:T(8,128)(2,1)S(1)} %get-tuple-element.19.split_ref, bf16[272,128]{1,0:T(8,128)(2,1)S(1)} %get-tuple-element.20.refs_0_, bf16[272,128]{1,0:T(8,128)(2,1)S(1)} %collective-permute-done.refs_1_, ...), custom_call_target="tpu_custom_call" | custom-call | tf_op jit(solution)/shard_map/pallas_call | solution.py:191
  16.8 0.0 collective-permute-done.6.refs_2_
  16.8 1.9 %collective-permute-done.8.weighted_b = f32[16,1024]{1,0:T(8,128)S(1)} collective-permute-done((f32[16,1024]{1,0:T(8,128)S(1)}, f32[16,1024]{1,0:T(8,128)S(1)}, u32[]{:S(2)}, u32[]{:S(2)}) %collective-permute-start.8) | collective-permute-done | bytes 65568 | tf_op jit(solution)/shard_map/ppermute | solution.py:259
  18.7 0.0 collective-permute-done.4.refs_0_
  18.7 0.0 collective-permute-done.5.refs_1_
  18.7 0.0 copy-start
  18.7 0.0 copy-start.1
  18.7 0.8 %shard_map.87 = f32[8,128]{1,0:T(8,128)S(1)} custom-call(f32[1,2]{1,0:T(1,128)S(1)} %get-tuple-element.18.harvest_ref, f32[16,1024]{1,0:T(8,128)S(1)} %add.6.weighted_a, f32[16,1024]{1,0:T(8,128)S(1)} %collective-permute-done.8.weighted_b, bf16[96,1024]{1,0:T(8,128)(2,1)S(1)} %get-tuple-element.19.split_ref, ...), custom_call_target="tpu_custom_call" | custom-call | tf_op jit(solution)/shard_map/pallas_call | solution.py:191
  19.5 2.6 %collective-permute-start.9 = (f32[8,128]{1,0:T(8,128)S(1)}, f32[8,128]{1,0:T(8,128)S(1)}, u32[]{:S(2)}, u32[]{:S(2)}) collective-permute-start(f32[8,128]{1,0:T(8,128)S(1)} %shard_map.87), channel_id=1, source_target_pairs={{0,16},{4,20},{8,24},{12,28},{16,0},{20,4},{24,8},{28,12},{1,17},{... | collective-permute-start | bytes 12296 | tf_op jit(solution)/shard_map/ppermute | solution.py:259
  22.1 2.0 %collective-permute-done.9 = f32[8,128]{1,0:T(8,128)S(1)} collective-permute-done((f32[8,128]{1,0:T(8,128)S(1)}, f32[8,128]{1,0:T(8,128)S(1)}, u32[]{:S(2)}, u32[]{:S(2)}) %collective-permute-start.9) | collective-permute-done | bytes 4128 | tf_op jit(solution)/shard_map/ppermute | solution.py:259
  24.0 1.5 %collective-permute-start.10 = (f32[8,128]{1,0:T(8,128)S(1)}, f32[8,128]{1,0:T(8,128)S(1)}, u32[]{:S(2)}, u32[]{:S(2)}) collective-permute-start(f32[8,128]{1,0:T(8,128)S(1)} %add.7.refs_0_), channel_id=1, source_target_pairs={{0,4},{4,0},{8,12},{12,8},{16,20},{20,16},{24,28},{28,24},{1,5},{5... | collective-permute-start | bytes 12296 | tf_op jit(solution)/shard_map/ppermute | solution.py:259
  25.5 0.9 %collective-permute-start.11 = (f32[8,128]{1,0:T(8,128)S(1)}, f32[8,128]{1,0:T(8,128)S(1)}, u32[]{:S(2)}, u32[]{:S(2)}) collective-permute-start(f32[8,128]{1,0:T(8,128)S(1)} %add.7.refs_0_), channel_id=1, source_target_pairs={{0,8},{4,12},{8,0},{12,4},{16,24},{20,28},{24,16},{28,20},{1,9},{5... | collective-permute-start | bytes 12296 | tf_op jit(solution)/shard_map/ppermute | solution.py:259
  26.3 1.2 %collective-permute-start.12 = (f32[8,128]{1,0:T(8,128)S(1)}, f32[8,128]{1,0:T(8,128)S(1)}, u32[]{:S(2)}, u32[]{:S(2)}) collective-permute-start(f32[8,128]{1,0:T(8,128)S(1)} %add.7.refs_0_), channel_id=1, source_target_pairs={{0,12},{4,8},{8,4},{12,0},{16,28},{20,24},{24,20},{28,16},{1,13},{... | collective-permute-start | bytes 12296 | tf_op jit(solution)/shard_map/ppermute | solution.py:259
  27.5 0.0 copy-done
  27.5 0.0 copy-done.1
  27.5 1.7 %shard_map.86 = (f32[2,16,1024]{2,1,0:T(8,128)}, f32[16,1024]{1,0:T(8,128)}) custom-call(f32[1,2]{1,0:T(1,128)S(1)} %get-tuple-element.18.harvest_ref, f32[2,16,1024]{2,1,0:T(8,128)S(1)} %copy-done, f32[16,1024]{1,0:T(8,128)S(1)} %copy-done.1, bf16[256,1024]{1,0:T(8,128)(2,1)S(1)} %get-tuple-element.24.placed_ref, ...), custom_call_target="tpu_custom_call" | custom-call | tf_op jit(solution)/shard_map/pallas_call | solution.py:191
  29.2 0.0 collective-permute-done.10.refs_1_
  29.2 0.0 collective-permute-done.11.refs_2_
  29.2 1.7 %collective-permute-done.12.refs_3_ = f32[8,128]{1,0:T(8,128)S(1)} collective-permute-done((f32[8,128]{1,0:T(8,128)S(1)}, f32[8,128]{1,0:T(8,128)S(1)}, u32[]{:S(2)}, u32[]{:S(2)}) %collective-permute-start.12) | collective-permute-done | bytes 4128 | tf_op jit(solution)/shard_map/ppermute | solution.py:259
  30.8 0.6 %shard_map.88 = (f32[2,16]{1,0:T(2,128)}, f32[1,16]{1,0:T(1,128)}) custom-call(f32[8,128]{1,0:T(8,128)S(1)} %add.7.refs_0_, f32[8,128]{1,0:T(8,128)S(1)} %collective-permute-done.10.refs_1_, f32[8,128]{1,0:T(8,128)S(1)} %collective-permute-done.11.refs_2_, f32[8,128]{1,0:T(8,128)S(1)} %collective-permute-done.12.refs_3_), custom_call_target="tpu_custom_call" | custom-call | tf_op jit(solution)/shard_map/pallas_call | solution.py:191
  (2 shorter events, 0.0 us)
Async XLA Ops:
  2.5 8.1 %collective-permute-start = (bf16[272,128]{1,0:T(8,128)(2,1)S(1)}, bf16[272,128]{1,0:T(8,128)(2,1)S(1)}, u32[]{:S(2)}, u32[]{:S(2)}) collective-permute-start(bf16[272,128]{1,0:T(8,128)(2,1)S(1)} %get-tuple-element.21), channel_id=1, source_target_pairs={{0,24},{1,21},{2,26},{3,23},{4,28},{5,17},{6,30},{7,19},{8,16},{9,... | collective-permute-start | bytes 208904 | tf_op jit(solution)/shard_map/ppermute | solution.py:227
  7.7 6.2 %collective-permute-start.1 = (bf16[272,128]{1,0:T(8,128)(2,1)S(1)}, bf16[272,128]{1,0:T(8,128)(2,1)S(1)}, u32[]{:S(2)}, u32[]{:S(2)}) collective-permute-start(bf16[272,128]{1,0:T(8,128)(2,1)S(1)} %get-tuple-element.22), channel_id=1, source_target_pairs={{0,8},{1,29},{2,10},{3,31},{4,12},{5,25},{6,14},{7,27},{8,0},{9,21... | collective-permute-start | bytes 208904 | tf_op jit(solution)/shard_map/ppermute | solution.py:227
  7.7 6.2 %collective-permute-start.2 = (bf16[272,128]{1,0:T(8,128)(2,1)S(1)}, bf16[272,128]{1,0:T(8,128)(2,1)S(1)}, u32[]{:S(2)}, u32[]{:S(2)}) collective-permute-start(bf16[272,128]{1,0:T(8,128)(2,1)S(1)} %get-tuple-element.23), channel_id=1, source_target_pairs={{0,16},{1,13},{2,18},{3,15},{4,20},{5,9},{6,22},{7,11},{8,24},{9,5... | collective-permute-start | bytes 208904 | tf_op jit(solution)/shard_map/ppermute | solution.py:227
  8.3 6.0 %collective-permute-start.7 = (f32[16,1024]{1,0:T(8,128)S(1)}, f32[16,1024]{1,0:T(8,128)S(1)}, u32[]{:S(2)}, u32[]{:S(2)}) collective-permute-start(f32[16,1024]{1,0:T(8,128)S(1)} %get-tuple-element.28), channel_id=1, source_target_pairs={{0,1},{1,0},{2,3},{3,2},{4,5},{5,4},{6,7},{7,6},{8,9},{9,8},{10,11... | collective-permute-start | bytes 196616 | tf_op jit(solution)/shard_map/ppermute | solution.py:259
  10.6 5.3 %collective-permute-start.3 = (bf16[272,128]{1,0:T(8,128)(2,1)S(1)}, bf16[272,128]{1,0:T(8,128)(2,1)S(1)}, u32[]{:S(2)}, u32[]{:S(2)}) collective-permute-start(bf16[272,128]{1,0:T(8,128)(2,1)S(1)} %collective-permute-done.refs_1_), channel_id=1, source_target_pairs={{0,1},{1,0},{2,3},{3,2},{4,5},{5,4},{6,7},{7,6},{8,9},{9,8},{10,11... | collective-permute-start | bytes 208904 | tf_op jit(solution)/shard_map/ppermute | solution.py:259
  10.6 6.1 %collective-permute-start.6 = (bf16[272,128]{1,0:T(8,128)(2,1)S(1)}, bf16[272,128]{1,0:T(8,128)(2,1)S(1)}, u32[]{:S(2)}, u32[]{:S(2)}) collective-permute-start(bf16[272,128]{1,0:T(8,128)(2,1)S(1)} %get-tuple-element.25), channel_id=1, source_target_pairs={{0,4},{1,5},{2,6},{3,7},{4,0},{5,1},{6,2},{7,3},{8,12},{9,13},{10,... | collective-permute-start | bytes 208904 | tf_op jit(solution)/shard_map/ppermute | solution.py:227
  13.8 4.9 %collective-permute-start.4 = (bf16[272,128]{1,0:T(8,128)(2,1)S(1)}, bf16[272,128]{1,0:T(8,128)(2,1)S(1)}, u32[]{:S(2)}, u32[]{:S(2)}) collective-permute-start(bf16[272,128]{1,0:T(8,128)(2,1)S(1)} %collective-permute-done.1.refs_2_), channel_id=1, source_target_pairs={{0,1},{1,0},{2,3},{3,2},{4,5},{5,4},{6,7},{7,6},{8,9},{9,8},{10,11... | collective-permute-start | bytes 208904 | tf_op jit(solution)/shard_map/ppermute | solution.py:259
  13.8 4.9 %collective-permute-start.5 = (bf16[272,128]{1,0:T(8,128)(2,1)S(1)}, bf16[272,128]{1,0:T(8,128)(2,1)S(1)}, u32[]{:S(2)}, u32[]{:S(2)}) collective-permute-start(bf16[272,128]{1,0:T(8,128)(2,1)S(1)} %collective-permute-done.2.refs_3_), channel_id=1, source_target_pairs={{0,1},{1,0},{2,3},{3,2},{4,5},{5,4},{6,7},{7,6},{8,9},{9,8},{10,11... | collective-permute-start | bytes 208904 | tf_op jit(solution)/shard_map/ppermute | solution.py:259
  14.4 4.3 %collective-permute-start.8 = (f32[16,1024]{1,0:T(8,128)S(1)}, f32[16,1024]{1,0:T(8,128)S(1)}, u32[]{:S(2)}, u32[]{:S(2)}) collective-permute-start(f32[16,1024]{1,0:T(8,128)S(1)} %add.6.weighted_a), channel_id=1, source_target_pairs={{0,2},{1,3},{2,0},{3,1},{4,6},{5,7},{6,4},{7,5},{8,10},{9,11},{10,... | collective-permute-start | bytes 196616 | tf_op jit(solution)/shard_map/ppermute | solution.py:259
  18.7 8.8 %copy-start = (f32[2,16,1024]{2,1,0:T(8,128)S(1)}, f32[2,16,1024]{2,1,0:T(8,128)}, u32[]{:S(2)}) copy-start(f32[2,16,1024]{2,1,0:T(8,128)} %density_ref.1) | copy-start | bytes 393220
  18.7 8.8 %copy-start.1 = (f32[16,1024]{1,0:T(8,128)S(1)}, f32[16,1024]{1,0:T(8,128)}, u32[]{:S(2)}) copy-start(f32[16,1024]{1,0:T(8,128)} %area_ref.1) | copy-start | bytes 196612
  19.5 4.5 %collective-permute-start.9 = (f32[8,128]{1,0:T(8,128)S(1)}, f32[8,128]{1,0:T(8,128)S(1)}, u32[]{:S(2)}, u32[]{:S(2)}) collective-permute-start(f32[8,128]{1,0:T(8,128)S(1)} %shard_map.87), channel_id=1, source_target_pairs={{0,16},{4,20},{8,24},{12,28},{16,0},{20,4},{24,8},{28,12},{1,17},{... | collective-permute-start | bytes 12296 | tf_op jit(solution)/shard_map/ppermute | solution.py:259
  24.0 5.1 %collective-permute-start.10 = (f32[8,128]{1,0:T(8,128)S(1)}, f32[8,128]{1,0:T(8,128)S(1)}, u32[]{:S(2)}, u32[]{:S(2)}) collective-permute-start(f32[8,128]{1,0:T(8,128)S(1)} %add.7.refs_0_), channel_id=1, source_target_pairs={{0,4},{4,0},{8,12},{12,8},{16,20},{20,16},{24,28},{28,24},{1,5},{5... | collective-permute-start | bytes 12296 | tf_op jit(solution)/shard_map/ppermute | solution.py:259
  25.5 3.7 %collective-permute-start.11 = (f32[8,128]{1,0:T(8,128)S(1)}, f32[8,128]{1,0:T(8,128)S(1)}, u32[]{:S(2)}, u32[]{:S(2)}) collective-permute-start(f32[8,128]{1,0:T(8,128)S(1)} %add.7.refs_0_), channel_id=1, source_target_pairs={{0,8},{4,12},{8,0},{12,4},{16,24},{20,28},{24,16},{28,20},{1,9},{5... | collective-permute-start | bytes 12296 | tf_op jit(solution)/shard_map/ppermute | solution.py:259
  26.3 4.5 %collective-permute-start.12 = (f32[8,128]{1,0:T(8,128)S(1)}, f32[8,128]{1,0:T(8,128)S(1)}, u32[]{:S(2)}, u32[]{:S(2)}) collective-permute-start(f32[8,128]{1,0:T(8,128)S(1)} %add.7.refs_0_), channel_id=1, source_target_pairs={{0,12},{4,8},{8,4},{12,0},{16,28},{20,24},{24,20},{28,16},{1,13},{... | collective-permute-start | bytes 12296 | tf_op jit(solution)/shard_map/ppermute | solution.py:259

commit v2 on v1

--- a/solution.py
+++ b/solution.py
@@ -59,7 +59,7 @@
     onehot = jnp.concatenate([matches(slots[k:k + 1], width) for k in range(count)], axis=0)
     high = lax.shift_right_logical(local, 7).astype(F32)
     low = (local & (LANES - 1)).astype(F32)
-    which = iota((16, owned), 0)
+    which = iota((8, owned), 0)
     extra = jnp.where(which == 0, high, jnp.where(which == 1, low, 0.0)).astype(BF16)
     for copy in copies[2:]:
         copy.wait()
@@ -213,7 +213,7 @@
     sources = (order.reshape(1, owned), fractions, harvest, density, area)
     *packed, weighted, split, harvest = call(
         functools.partial(pack_kernel, even=even, odd=odd),
-        [array(kinds + 16, chunk, dtype=BF16)] * count
+        [array(kinds + 8, chunk, dtype=BF16)] * count
         + [array(types, owned), array(3 * pools * types, owned, dtype=BF16), array(1, pools)],
         [pltpu.with_memory_space_constraint(x, pltpu.HBM) for x in sources],
         scratch=[pltpu.VMEM(x.shape, x.dtype) for x in sources] + [pltpu.SemaphoreType.DMA((len(sources),))],
@@ -259,7 +259,7 @@
     return lax.ppermute(value, axis, [(n, n ^ step) for n in range(size)])
 
 
-SPLIT = {8: ((6, 2, 4, 1), (5, 7, 3, 1))}
+SPLIT = {8: ((6, 4, 2, 1), (5, 7, 3, 1))}
 EARLY = 1
 
 

time: 31.6 us -> 31.4 us (level)
  starting transfers between devices: 15.6 us -> 15.1 us
  waiting for transfers between devices: 9.31 us -> 9.63 us
    ppermute x9, starting transfers between devices: 8.19 us -> 7.74 us  [swap(): return lax.ppermute(value, axis, [(n, n ^ step) for n in range(size)])]
    ppermute x4, waiting for transfers between devices: 3.77 us -> 4.11 us  [fast_body(): received.append(lax.ppermute(packed[1 + k], ('cell', 'pool'), pairs))]
where the time goes in v2:
time: 31.4 us; the launch traced here: 31.2 us
  starting transfers between devices  15.1 us (48%)
  waiting for transfers between devices  9.63 us (31%)
  Pallas kernels  5.74 us (18%)
  between operations  0.69 us (2%)
    ppermute x9, starting transfers between devices, swap(): return lax.ppermute(value, axis, [(n, n ^ step) for n in range(size)])  7.74 us
    ppermute x4, starting transfers between devices, fast_body(): received.append(lax.ppermute(packed[1 + k], ('cell', 'pool'), pairs))  7.4 us
    pallas_call x5, Pallas kernels, call(): pl.pallas_call(kernel, out_shape=out_shape, in_specs=[pl.BlockSpec(memory...  5.74 us
    ppermute x9, waiting for transfers between devices, swap(): return lax.ppermute(value, axis, [(n, n ^ step) for n in range(size)])  5.52 us
    ppermute x4, waiting for transfers between devices, fast_body(): received.append(lax.ppermute(packed[1 + k], ('cell', 'pool'), pairs))  4.11 us
  transfers between devices with their start and end apart: 13, of which 5 were waited for; matrix products, arithmetic and copies ran while one was open for 0% of the time, Pallas kernels for 8%

profile of v2, /device:TPU:0, one launch (start us, length us, event | category | flops | bytes accessed | tf_op | source)
XLA Modules:
  0.0 31.2 jit_solution(9488701878806170706)
XLA Ops:
  0.6 1.9 %shard_map.84 = (bf16[264,128]{1,0:T(8,128)(2,1)S(1)}, bf16[264,128]{1,0:T(8,128)(2,1)S(1)}, bf16[264,128]{1,0:T(8,128)(2,1)S(1)}, bf16[264,128]{1,0:T(8,128)(2,...) custom-call(s32[1,1024]{1,0:T(1,128)} %bitcast.3, ...), custom_call_target="tpu_custom_call" | custom-call | tf_op jit(solution)/shard_map/pallas_call | solution.py:191
  2.5 5.1 %collective-permute-start = (bf16[264,128]{1,0:T(8,128)(2,1)S(1)}, bf16[264,128]{1,0:T(8,128)(2,1)S(1)}, u32[]{:S(2)}, u32[]{:S(2)}) collective-permute-start(bf16[264,128]{1,0:T(8,128)(2,1)S(1)} %get-tuple-element.21), channel_id=1, source_target_pairs={{0,24},{1,21},{2,26},{3,23},{4,28},{5,17},{6,30},{7,19},{8,16},{9,... | collective-permute-start | bytes 202760 | tf_op jit(solution)/shard_map/ppermute | solution.py:227
  7.6 0.0 collective-permute-start.1
  7.7 0.6 %collective-permute-start.2 = (bf16[264,128]{1,0:T(8,128)(2,1)S(1)}, bf16[264,128]{1,0:T(8,128)(2,1)S(1)}, u32[]{:S(2)}, u32[]{:S(2)}) collective-permute-start(bf16[264,128]{1,0:T(8,128)(2,1)S(1)} %get-tuple-element.23), channel_id=1, source_target_pairs={{0,8},{1,13},{2,10},{3,15},{4,12},{5,9},{6,14},{7,11},{8,0},{9,5},... | collective-permute-start | bytes 202760 | tf_op jit(solution)/shard_map/ppermute | solution.py:227
  8.3 0.1 collective-permute-start.7
  8.4 2.2 %collective-permute-done.refs_1_ = bf16[264,128]{1,0:T(8,128)(2,1)S(1)} collective-permute-done((bf16[264,128]{1,0:T(8,128)(2,1)S(1)}, bf16[264,128]{1,0:T(8,128)(2,1)S(1)}, u32[]{:S(2)}, u32[]{:S(2)}) %collective-permute-start) | collective-permute-done | bytes 67616 | tf_op jit(solution)/shard_map/ppermute | solution.py:227
  10.6 0.0 collective-permute-start.3
  10.6 1.6 %collective-permute-start.6 = (bf16[264,128]{1,0:T(8,128)(2,1)S(1)}, bf16[264,128]{1,0:T(8,128)(2,1)S(1)}, u32[]{:S(2)}, u32[]{:S(2)}) collective-permute-start(bf16[264,128]{1,0:T(8,128)(2,1)S(1)} %get-tuple-element.25), channel_id=1, source_target_pairs={{0,4},{1,5},{2,6},{3,7},{4,0},{5,1},{6,2},{7,3},{8,12},{9,13},{10,... | collective-permute-start | bytes 202760 | tf_op jit(solution)/shard_map/ppermute | solution.py:227
  12.2 1.9 %collective-permute-done.1.refs_2_ = bf16[264,128]{1,0:T(8,128)(2,1)S(1)} collective-permute-done((bf16[264,128]{1,0:T(8,128)(2,1)S(1)}, bf16[264,128]{1,0:T(8,128)(2,1)S(1)}, u32[]{:S(2)}, u32[]{:S(2)}) %collective-permute-start.1) | collective-permute-done | bytes 67616 | tf_op jit(solution)/shard_map/ppermute | solution.py:227
  14.1 0.0 collective-permute-start.4
  14.1 0.0 collective-permute-done.2.refs_3_
  14.1 0.5 %collective-permute-start.5 = (bf16[264,128]{1,0:T(8,128)(2,1)S(1)}, bf16[264,128]{1,0:T(8,128)(2,1)S(1)}, u32[]{:S(2)}, u32[]{:S(2)}) collective-permute-start(bf16[264,128]{1,0:T(8,128)(2,1)S(1)} %collective-permute-done.2.refs_3_), channel_id=1, source_target_pairs={{0,1},{1,0},{2,3},{3,2},{4,5},{5,4},{6,7},{7,6},{8,9},{9,8},{10,11... | collective-permute-start | bytes 202760 | tf_op jit(solution)/shard_map/ppermute | solution.py:259
  14.6 0.0 collective-permute-done.7
  14.7 1.6 %collective-permute-start.8 = (f32[16,1024]{1,0:T(8,128)S(1)}, f32[16,1024]{1,0:T(8,128)S(1)}, u32[]{:S(2)}, u32[]{:S(2)}) collective-permute-start(f32[16,1024]{1,0:T(8,128)S(1)} %add.6.weighted_a), channel_id=1, source_target_pairs={{0,2},{1,3},{2,0},{3,1},{4,6},{5,7},{6,4},{7,5},{8,10},{9,11},{10,... | collective-permute-start | bytes 196616 | tf_op jit(solution)/shard_map/ppermute | solution.py:259
  16.2 0.0 collective-permute-done.3.refs_4_
  16.2 0.9 %shard_map.85 = (bf16[256,1024]{1,0:T(8,128)(2,1)S(1)}, f32[256,96]{1,0:T(8,128)S(1)}) custom-call(bf16[96,1024]{1,0:T(8,128)(2,1)S(1)} %get-tuple-element.19.split_ref, bf16[264,128]{1,0:T(8,128)(2,1)S(1)} %get-tuple-element.20.refs_0_, bf16[264,128]{1,0:T(8,128)(2,1)S(1)} %collective-permute-done.refs_1_, ...), custom_call_target="tpu_custom_call" | custom-call | tf_op jit(solution)/shard_map/pallas_call | solution.py:191
  17.1 0.0 collective-permute-done.6.refs_2_
  17.1 1.9 %collective-permute-done.8.weighted_b = f32[16,1024]{1,0:T(8,128)S(1)} collective-permute-done((f32[16,1024]{1,0:T(8,128)S(1)}, f32[16,1024]{1,0:T(8,128)S(1)}, u32[]{:S(2)}, u32[]{:S(2)}) %collective-permute-start.8) | collective-permute-done | bytes 65568 | tf_op jit(solution)/shard_map/ppermute | solution.py:259
  19.0 0.0 collective-permute-done.4.refs_0_
  19.0 0.0 collective-permute-done.5.refs_1_
  19.0 0.0 copy-start
  19.0 0.0 copy-start.1
  19.0 0.8 %shard_map.87 = f32[8,128]{1,0:T(8,128)S(1)} custom-call(f32[1,2]{1,0:T(1,128)S(1)} %get-tuple-element.18.harvest_ref, f32[16,1024]{1,0:T(8,128)S(1)} %add.6.weighted_a, f32[16,1024]{1,0:T(8,128)S(1)} %collective-permute-done.8.weighted_b, bf16[96,1024]{1,0:T(8,128)(2,1)S(1)} %get-tuple-element.19.split_ref, ...), custom_call_target="tpu_custom_call" | custom-call | tf_op jit(solution)/shard_map/pallas_call | solution.py:191
  19.8 2.1 %collective-permute-start.9 = (f32[8,128]{1,0:T(8,128)S(1)}, f32[8,128]{1,0:T(8,128)S(1)}, u32[]{:S(2)}, u32[]{:S(2)}) collective-permute-start(f32[8,128]{1,0:T(8,128)S(1)} %shard_map.87), channel_id=1, source_target_pairs={{0,16},{4,20},{8,24},{12,28},{16,0},{20,4},{24,8},{28,12},{1,17},{... | collective-permute-start | bytes 12296 | tf_op jit(solution)/shard_map/ppermute | solution.py:259
  21.9 2.4 %collective-permute-done.9 = f32[8,128]{1,0:T(8,128)S(1)} collective-permute-done((f32[8,128]{1,0:T(8,128)S(1)}, f32[8,128]{1,0:T(8,128)S(1)}, u32[]{:S(2)}, u32[]{:S(2)}) %collective-permute-start.9) | collective-permute-done | bytes 4128 | tf_op jit(solution)/shard_map/ppermute | solution.py:259
  24.3 1.0 %collective-permute-start.10 = (f32[8,128]{1,0:T(8,128)S(1)}, f32[8,128]{1,0:T(8,128)S(1)}, u32[]{:S(2)}, u32[]{:S(2)}) collective-permute-start(f32[8,128]{1,0:T(8,128)S(1)} %add.7.refs_0_), channel_id=1, source_target_pairs={{0,4},{4,0},{8,12},{12,8},{16,20},{20,16},{24,28},{28,24},{1,5},{5... | collective-permute-start | bytes 12296 | tf_op jit(solution)/shard_map/ppermute | solution.py:259
  25.3 0.8 %collective-permute-start.11 = (f32[8,128]{1,0:T(8,128)S(1)}, f32[8,128]{1,0:T(8,128)S(1)}, u32[]{:S(2)}, u32[]{:S(2)}) collective-permute-start(f32[8,128]{1,0:T(8,128)S(1)} %add.7.refs_0_), channel_id=1, source_target_pairs={{0,8},{4,12},{8,0},{12,4},{16,24},{20,28},{24,16},{28,20},{1,9},{5... | collective-permute-start | bytes 12296 | tf_op jit(solution)/shard_map/ppermute | solution.py:259
  26.1 1.7 %collective-permute-start.12 = (f32[8,128]{1,0:T(8,128)S(1)}, f32[8,128]{1,0:T(8,128)S(1)}, u32[]{:S(2)}, u32[]{:S(2)}) collective-permute-start(f32[8,128]{1,0:T(8,128)S(1)} %add.7.refs_0_), channel_id=1, source_target_pairs={{0,12},{4,8},{8,4},{12,0},{16,28},{20,24},{24,20},{28,16},{1,13},{... | collective-permute-start | bytes 12296 | tf_op jit(solution)/shard_map/ppermute | solution.py:259
  27.8 0.0 copy-done
  27.8 0.0 copy-done.1
  27.8 1.6 %shard_map.86 = (f32[2,16,1024]{2,1,0:T(8,128)}, f32[16,1024]{1,0:T(8,128)}) custom-call(f32[1,2]{1,0:T(1,128)S(1)} %get-tuple-element.18.harvest_ref, f32[2,16,1024]{2,1,0:T(8,128)S(1)} %copy-done, f32[16,1024]{1,0:T(8,128)S(1)} %copy-done.1, bf16[256,1024]{1,0:T(8,128)(2,1)S(1)} %get-tuple-element.24.placed_ref, ...), custom_call_target="tpu_custom_call" | custom-call | tf_op jit(solution)/shard_map/pallas_call | solution.py:191
  29.5 0.0 collective-permute-done.10.refs_1_
  29.5 0.0 collective-permute-done.11.refs_2_
  29.5 1.2 %collective-permute-done.12.refs_3_ = f32[8,128]{1,0:T(8,128)S(1)} collective-permute-done((f32[8,128]{1,0:T(8,128)S(1)}, f32[8,128]{1,0:T(8,128)S(1)}, u32[]{:S(2)}, u32[]{:S(2)}) %collective-permute-start.12) | collective-permute-done | bytes 4128 | tf_op jit(solution)/shard_map/ppermute | solution.py:259
  30.7 0.6 %shard_map.88 = (f32[2,16]{1,0:T(2,128)}, f32[1,16]{1,0:T(1,128)}) custom-call(f32[8,128]{1,0:T(8,128)S(1)} %add.7.refs_0_, f32[8,128]{1,0:T(8,128)S(1)} %collective-permute-done.10.refs_1_, f32[8,128]{1,0:T(8,128)S(1)} %collective-permute-done.11.refs_2_, f32[8,128]{1,0:T(8,128)S(1)} %collective-permute-done.12.refs_3_), custom_call_target="tpu_custom_call" | custom-call | tf_op jit(solution)/shard_map/pallas_call | solution.py:191
  (2 shorter events, 0.0 us)
Async XLA Ops:
  2.5 8.1 %collective-permute-start = (bf16[264,128]{1,0:T(8,128)(2,1)S(1)}, bf16[264,128]{1,0:T(8,128)(2,1)S(1)}, u32[]{:S(2)}, u32[]{:S(2)}) collective-permute-start(bf16[264,128]{1,0:T(8,128)(2,1)S(1)} %get-tuple-element.21), channel_id=1, source_target_pairs={{0,24},{1,21},{2,26},{3,23},{4,28},{5,17},{6,30},{7,19},{8,16},{9,... | collective-permute-start | bytes 202760 | tf_op jit(solution)/shard_map/ppermute | solution.py:227
  7.6 6.5 %collective-permute-start.1 = (bf16[264,128]{1,0:T(8,128)(2,1)S(1)}, bf16[264,128]{1,0:T(8,128)(2,1)S(1)}, u32[]{:S(2)}, u32[]{:S(2)}) collective-permute-start(bf16[264,128]{1,0:T(8,128)(2,1)S(1)} %get-tuple-element.22), channel_id=1, source_target_pairs={{0,16},{1,29},{2,18},{3,31},{4,20},{5,25},{6,22},{7,27},{8,24},{9,... | collective-permute-start | bytes 202760 | tf_op jit(solution)/shard_map/ppermute | solution.py:227
  7.7 6.5 %collective-permute-start.2 = (bf16[264,128]{1,0:T(8,128)(2,1)S(1)}, bf16[264,128]{1,0:T(8,128)(2,1)S(1)}, u32[]{:S(2)}, u32[]{:S(2)}) collective-permute-start(bf16[264,128]{1,0:T(8,128)(2,1)S(1)} %get-tuple-element.23), channel_id=1, source_target_pairs={{0,8},{1,13},{2,10},{3,15},{4,12},{5,9},{6,14},{7,11},{8,0},{9,5},... | collective-permute-start | bytes 202760 | tf_op jit(solution)/shard_map/ppermute | solution.py:227
  8.3 6.3 %collective-permute-start.7 = (f32[16,1024]{1,0:T(8,128)S(1)}, f32[16,1024]{1,0:T(8,128)S(1)}, u32[]{:S(2)}, u32[]{:S(2)}) collective-permute-start(f32[16,1024]{1,0:T(8,128)S(1)} %get-tuple-element.28), channel_id=1, source_target_pairs={{0,1},{1,0},{2,3},{3,2},{4,5},{5,4},{6,7},{7,6},{8,9},{9,8},{10,11... | collective-permute-start | bytes 196616 | tf_op jit(solution)/shard_map/ppermute | solution.py:259
  10.6 5.6 %collective-permute-start.3 = (bf16[264,128]{1,0:T(8,128)(2,1)S(1)}, bf16[264,128]{1,0:T(8,128)(2,1)S(1)}, u32[]{:S(2)}, u32[]{:S(2)}) collective-permute-start(bf16[264,128]{1,0:T(8,128)(2,1)S(1)} %collective-permute-done.refs_1_), channel_id=1, source_target_pairs={{0,1},{1,0},{2,3},{3,2},{4,5},{5,4},{6,7},{7,6},{8,9},{9,8},{10,11... | collective-permute-start | bytes 202760 | tf_op jit(solution)/shard_map/ppermute | solution.py:259
  10.6 6.5 %collective-permute-start.6 = (bf16[264,128]{1,0:T(8,128)(2,1)S(1)}, bf16[264,128]{1,0:T(8,128)(2,1)S(1)}, u32[]{:S(2)}, u32[]{:S(2)}) collective-permute-start(bf16[264,128]{1,0:T(8,128)(2,1)S(1)} %get-tuple-element.25), channel_id=1, source_target_pairs={{0,4},{1,5},{2,6},{3,7},{4,0},{5,1},{6,2},{7,3},{8,12},{9,13},{10,... | collective-permute-start | bytes 202760 | tf_op jit(solution)/shard_map/ppermute | solution.py:227
  14.1 4.9 %collective-permute-start.4 = (bf16[264,128]{1,0:T(8,128)(2,1)S(1)}, bf16[264,128]{1,0:T(8,128)(2,1)S(1)}, u32[]{:S(2)}, u32[]{:S(2)}) collective-permute-start(bf16[264,128]{1,0:T(8,128)(2,1)S(1)} %collective-permute-done.1.refs_2_), channel_id=1, source_target_pairs={{0,1},{1,0},{2,3},{3,2},{4,5},{5,4},{6,7},{7,6},{8,9},{9,8},{10,11... | collective-permute-start | bytes 202760 | tf_op jit(solution)/shard_map/ppermute | solution.py:259
  14.1 4.9 %collective-permute-start.5 = (bf16[264,128]{1,0:T(8,128)(2,1)S(1)}, bf16[264,128]{1,0:T(8,128)(2,1)S(1)}, u32[]{:S(2)}, u32[]{:S(2)}) collective-permute-start(bf16[264,128]{1,0:T(8,128)(2,1)S(1)} %collective-permute-done.2.refs_3_), channel_id=1, source_target_pairs={{0,1},{1,0},{2,3},{3,2},{4,5},{5,4},{6,7},{7,6},{8,9},{9,8},{10,11... | collective-permute-start | bytes 202760 | tf_op jit(solution)/shard_map/ppermute | solution.py:259
  14.7 4.3 %collective-permute-start.8 = (f32[16,1024]{1,0:T(8,128)S(1)}, f32[16,1024]{1,0:T(8,128)S(1)}, u32[]{:S(2)}, u32[]{:S(2)}) collective-permute-start(f32[16,1024]{1,0:T(8,128)S(1)} %add.6.weighted_a), channel_id=1, source_target_pairs={{0,2},{1,3},{2,0},{3,1},{4,6},{5,7},{6,4},{7,5},{8,10},{9,11},{10,... | collective-permute-start | bytes 196616 | tf_op jit(solution)/shard_map/ppermute | solution.py:259
  19.0 8.8 %copy-start = (f32[2,16,1024]{2,1,0:T(8,128)S(1)}, f32[2,16,1024]{2,1,0:T(8,128)}, u32[]{:S(2)}) copy-start(f32[2,16,1024]{2,1,0:T(8,128)} %density_ref.1) | copy-start | bytes 393220
  19.0 8.8 %copy-start.1 = (f32[16,1024]{1,0:T(8,128)S(1)}, f32[16,1024]{1,0:T(8,128)}, u32[]{:S(2)}) copy-start(f32[16,1024]{1,0:T(8,128)} %area_ref.1) | copy-start | bytes 196612
  19.8 4.5 %collective-permute-start.9 = (f32[8,128]{1,0:T(8,128)S(1)}, f32[8,128]{1,0:T(8,128)S(1)}, u32[]{:S(2)}, u32[]{:S(2)}) collective-permute-start(f32[8,128]{1,0:T(8,128)S(1)} %shard_map.87), channel_id=1, source_target_pairs={{0,16},{4,20},{8,24},{12,28},{16,0},{20,4},{24,8},{28,12},{1,17},{... | collective-permute-start | bytes 12296 | tf_op jit(solution)/shard_map/ppermute | solution.py:259
  24.3 5.1 %collective-permute-start.10 = (f32[8,128]{1,0:T(8,128)S(1)}, f32[8,128]{1,0:T(8,128)S(1)}, u32[]{:S(2)}, u32[]{:S(2)}) collective-permute-start(f32[8,128]{1,0:T(8,128)S(1)} %add.7.refs_0_), channel_id=1, source_target_pairs={{0,4},{4,0},{8,12},{12,8},{16,20},{20,16},{24,28},{28,24},{1,5},{5... | collective-permute-start | bytes 12296 | tf_op jit(solution)/shard_map/ppermute | solution.py:259
  25.3 4.2 %collective-permute-start.11 = (f32[8,128]{1,0:T(8,128)S(1)}, f32[8,128]{1,0:T(8,128)S(1)}, u32[]{:S(2)}, u32[]{:S(2)}) collective-permute-start(f32[8,128]{1,0:T(8,128)S(1)} %add.7.refs_0_), channel_id=1, source_target_pairs={{0,8},{4,12},{8,0},{12,4},{16,24},{20,28},{24,16},{28,20},{1,9},{5... | collective-permute-start | bytes 12296 | tf_op jit(solution)/shard_map/ppermute | solution.py:259
  26.1 4.5 %collective-permute-start.12 = (f32[8,128]{1,0:T(8,128)S(1)}, f32[8,128]{1,0:T(8,128)S(1)}, u32[]{:S(2)}, u32[]{:S(2)}) collective-permute-start(f32[8,128]{1,0:T(8,128)S(1)} %add.7.refs_0_), channel_id=1, source_target_pairs={{0,12},{4,8},{8,4},{12,0},{16,28},{20,24},{24,20},{28,16},{1,13},{... | collective-permute-start | bytes 12296 | tf_op jit(solution)/shard_map/ppermute | solution.py:259
